TPU v7x, 32 devices: a whole 2x2x4 slice. The times are simulated.
32 devices in a mesh: win: 2 (over core), grp: 16 (over z, y, x).
Axes of the slice: x: 2, y: 2, z: 4, core: 2. Of those that a mesh axis runs over, the one named last changes fastest.
Arguments:
- atom_table: float32 [4, 6, 24576], P('win', None, 'grp'), as said below
- row_blocks: int32 [4, 1024], P('win', 'grp'), may hold values from 0 to 191, as said below
- col_blocks: int32 [4, 1024], P('win', 'grp'), may hold values from 0 to 191, as said below
- lambdas: float32 [4], replicated, may hold values from 0 to 1, as said below
- inverse_temp: float32 [1], replicated, may hold values from 20 to 80
- parity: int32 [1], replicated, may hold values from 0 to 1073741823
- thresholds: int32 [4], replicated, may hold values from 0 to 1073741823
Outputs:
- energies: float32 [4, 3], P('win')
- margins: float32 [4], P('win')
- profile: float32 [4], P('win')
Inputs may be any that keep to these rules, and one draw needn't show every extreme that they name: `row_blocks`: the first block of each pair listed on index g of grp lies in that index's share of atoms: blocks g * 12 to (g + 1) * 12 - 1. `col_blocks`: the list of one index of grp names blocks of any one index of grp (itself included) at most 5 times; in each window some index of grp has exactly 5 of its blocks named in every list of that window. `lambdas`: strictly increasing. `atom_table`: field 4 lies in 0.7 to 1.4 and field 5 in 0.6 to 1.4.
All inputs are finite; a program needn't handle non-finite values.
Results may differ from a plain program's by a relative error of at most 0.0003.
Values sent between devices are 32-bit elements; how exact they have to be, the bound alone decides.
A program may use at most 64 MiB of HBM per device.

v0:
```python
import jax
import jax.numpy as jnp
from jax import lax
from jax.sharding import PartitionSpec as P

TILE = 128


tiles_per_step = 16


def from_behind(shard, axis, by):
    peers = lax.axis_size(axis)
    pairs = [(i, i + by) for i in range(peers) if 0 <= i + by < peers]
    return lax.ppermute(shard, axis, pairs)


def entering(part, axis, combine, identity):
    place = lax.axis_index(axis)
    gathered = lax.all_gather(part, axis)
    state = jnp.zeros_like(part) + jnp.asarray(identity, part.dtype)

    def one(step, state):
        return combine(state, lax.dynamic_index_in_dim(gathered, step, 0, False))

    return lax.fori_loop(0, place, one, state)


def pair_energy(row_data, col_data, same_block, lambda_set):
    delta_x = row_data[0][:, :, None] - col_data[0][:, None, :]
    delta_y = row_data[1][:, :, None] - col_data[1][:, None, :]
    delta_z = row_data[2][:, :, None] - col_data[2][:, None, :]
    distance = delta_x * delta_x + delta_y * delta_y + delta_z * delta_z
    charge_pair = row_data[3][:, :, None] * col_data[3][:, None, :]
    well_depth = 4.0 * row_data[4][:, :, None] * col_data[4][:, None, :]
    size_pair = row_data[5][:, :, None] * col_data[5][:, None, :]
    scaled = distance / size_pair
    scaled_cube = scaled * scaled * scaled
    width_tile = distance.shape[-1]
    diagonal = (
        lax.broadcasted_iota(jnp.int32, (width_tile, width_tile), 0)
        == lax.broadcasted_iota(jnp.int32, (width_tile, width_tile), 1)
    ).astype(jnp.float32)
    keep_mask = 1.0 - same_block[:, None, None] * diagonal[None]
    totals = []
    for number in range(3):
        lam_now = lambda_set[number]
        softened = 1.0 - 0.5 * lam_now + scaled_cube
        inverse = 1.0 / softened
        dispersion = well_depth * (inverse * inverse - inverse)
        coulomb = charge_pair * lax.rsqrt(distance + 2.0 - lam_now)
        totals.append(lam_now * jnp.sum(keep_mask * (dispersion + coulomb)))
    return jnp.stack(totals)


def evaluate(row_all, col_all, same_all, lambda_set):
    count = same_all.shape[0] // tiles_per_step

    def advance(number, total):
        start = number * tiles_per_step
        row_part = lax.dynamic_slice_in_dim(row_all, start, tiles_per_step, 1)
        col_part = lax.dynamic_slice_in_dim(col_all, start, tiles_per_step, 1)
        same_part = lax.dynamic_slice_in_dim(same_all, start, tiles_per_step, 0)
        return total + pair_energy(row_part, col_part, same_part, lambda_set)

    return lax.fori_loop(0, count, advance, jnp.zeros((3,), jnp.float32))


def add_terms(earlier, later):
    return earlier + later


def take_blocks(source, indices):
    return jnp.take(source, indices, axis=1)


def per_device(atom_table, row_blocks, col_blocks, lambdas, inverse_temp, parity, thresholds):
    windows = lax.axis_size("win") * atom_table.shape[0]
    groups = lax.axis_size("grp")
    window_run = atom_table.shape[0]
    member = lax.axis_index("grp")
    first_window = lax.axis_index("win") * window_run
    fields = atom_table.shape[1]
    blocks_own = atom_table.reshape(window_run, fields, -1, TILE)
    own_count = blocks_own.shape[2]
    listed = row_blocks.shape[1]
    row_data = jax.vmap(take_blocks)(blocks_own, row_blocks - member * own_count)
    slot_count = max(2, 5 * listed // (4 * groups))
    peers = jnp.arange(groups, dtype=jnp.int32)
    slot_ids = jnp.arange(slot_count, dtype=jnp.int32)

    def plan(col_ids):
        owner_ids = col_ids // own_count
        within_ids = col_ids - owner_ids * own_count
        owner_hot = (owner_ids[:, None] == peers[None, :]).astype(jnp.int32)
        earlier_hot = jnp.cumsum(owner_hot, axis=0) - owner_hot
        order_rank = jnp.sum(earlier_hot * owner_hot, axis=1)
        matched = owner_hot[:, :, None] * (
            order_rank[:, None, None] == slot_ids[None, None, :]
        ).astype(jnp.int32)
        requests = jnp.sum(matched * (within_ids + 1)[:, None, None], axis=0) - 1
        return (owner_ids * slot_count + order_rank, requests)

    positions, requests = jax.vmap(plan)(col_blocks)
    incoming = lax.all_to_all(requests, "grp", split_axis=1, concat_axis=1, tiled=True)

    def answer(source, asked):
        picked = jnp.take(source, jnp.maximum(asked, 0), axis=1)
        return jnp.where((asked >= 0)[None, :, :, None], picked, 0.0)

    replies = jax.vmap(answer)(blocks_own, incoming)
    returned = lax.all_to_all(replies, "grp", split_axis=2, concat_axis=2, tiled=True)
    flat_back = returned.reshape(window_run, fields, groups * slot_count, TILE)
    col_data = jax.vmap(take_blocks)(flat_back, positions)
    same_all = (row_blocks == col_blocks).astype(jnp.float32)
    window = first_window + jnp.arange(window_run, dtype=jnp.int32)
    below = jnp.maximum(window - 1, 0)
    above = jnp.minimum(window + 1, windows - 1)
    lambda_sets = jnp.stack([lambdas[below], lambdas[window], lambdas[above]], axis=1)
    partial_sums = lax.map(
        lambda pack: evaluate(pack[0], pack[1], pack[2], pack[3]),
        (row_data, col_data, same_all, lambda_sets),
    )
    scale_count = listed * groups * TILE * TILE
    lower_win = jnp.where(jnp.remainder(window - parity[0], 2) == 0, window, window - 1)
    upper_win = lower_win + 1
    has_partner = (lower_win >= 0) & (upper_win < windows)
    lower_safe = jnp.clip(lower_win, 0, windows - 1)
    summed = lax.psum(partial_sums, "grp")
    energy = summed / scale_count
    d_plus = energy[:, 2] - energy[:, 1]
    d_minus = energy[:, 0] - energy[:, 1]
    minus_above = from_behind(d_minus[0:1], "win", -1)
    plus_below = from_behind(d_plus[window_run - 1 : window_run], "win", 1)
    minus_next = jnp.concatenate([d_minus[1:], minus_above])
    plus_prev = jnp.concatenate([plus_below, d_plus[:-1]])
    change = jnp.where(lower_win == window, d_plus + minus_next, plus_prev + d_minus)
    carried = entering(jnp.sum(d_plus)[None], "win", add_terms, jnp.zeros((1,), jnp.float32))
    profile = carried + (jnp.cumsum(d_plus) - d_plus)
    offset_draw = jnp.remainder(thresholds[lower_safe] + parity[0], 1073741824) + 1
    draw_share = offset_draw.astype(jnp.float32) / 1073741824.0
    margins = jnp.where(has_partner, -jnp.log(draw_share) - inverse_temp[0] * change, 0.0)
    return (energy, margins, profile)


def solution(mesh):
    return jax.shard_map(
        per_device,
        mesh=mesh,
        in_specs=(P("win", None, "grp"), P("win", "grp"), P("win", "grp"), P(), P(), P(), P()),
        out_specs=(P("win", None), P("win"), P("win")),
        check_vma=False,
    )
```

profile of v0, /device:TPU:0, one launch (start us, length us, event | category | flops | bytes accessed | tf_op | source)
XLA Modules:
  0.0 196.2 jit_solution(12268638286886576941)
XLA Ops:
  2.8 8.3 %all-to-all-start = ((s32[2,16,5]{2,0,1:T(2,128)}), s32[2,16,5]{2,0,1:T(2,128)S(1)}, u32[]{:S(2)}, u32[]{:S(2)}) async-start(s32[2,16,5]{2,0,1:T(2,128)} %copy.51), calls=%async_computation | async-start | bytes 32768 | tf_op jit(solution)/shard_map/all_to_all | solution.py:105
  12.6 5.8 %all-to-all-done = s32[2,16,5]{2,0,1:T(2,128)S(1)} async-done(((s32[2,16,5]{2,0,1:T(2,128)}), s32[2,16,5]{2,0,1:T(2,128)S(1)}, u32[]{:S(2)}, u32[]{:S(2)}) %all-to-all-start) | async-done | bytes 672 | tf_op jit(solution)/shard_map/all_to_all | solution.py:105
  22.2 3.6 %all-to-all-start.1 = ((f32[2,6,16,5,128]{4,0,3,1,2:T(2,128)}), f32[2,6,16,5,128]{4,0,3,1,2:T(2,128)S(1)}, u32[]{:S(2)}, u32[]{:S(2)}) async-start(f32[2,6,16,5,128]{4,0,3,1,2:T(2,128)} %copy.58), calls=%async_computation.1 | async-start | bytes 983040 | tf_op jit(solution)/shard_map/all_to_all | solution.py:112
  31.8 7.3 %all-to-all-done.1 = f32[2,6,16,5,128]{4,0,3,1,2:T(2,128)S(1)} async-done(((f32[2,6,16,5,128]{4,0,3,1,2:T(2,128)}), f32[2,6,16,5,128]{4,0,3,1,2:T(2,128)S(1)}, u32[]{:S(2)}, u32[]{:S(2)}) %all-to-all-start.1) | async-done | bytes 491552 | tf_op jit(solution)/shard_map/all_to_all | solution.py:112
  40.7 102.3 %while.37 = (s32[]{:T(128)}, f32[2,3]{1,0:T(2,128)S(1)}, f32[2,6,64,128]{3,2,0,1:T(8,128)S(1)}, f32[2,6,64,128]{3,2,0,1:T(8,128)S(1)}, f32[2,64]{1,0:T(2,128)S(1...) while((s32[]{:T(128)}, f32[2,3]{1,0:T(2,128)S(1)}, ...), condition=%wide.region_9.10_spmd, body=%wide.region_3.0_spmd.sunk | while | flops 16812060 | bytes 1377978 | solution.py:120
  43.4 48.4 %while.39 = (s32[]{:T(128)}, f32[3]{0:T(128)S(1)}, f32[3]{0:T(128)S(1)}, f32[64]{0:T(128)S(1)}, f32[6,64,128]{2,1,0:T(8,128)S(1)}, /*index=5*/f32[6,64,128]{2,1,...) while((s32[]{:T(128)}, f32[3]{0:T(128)S(1)}, ...), condition=%wide.region_8.8_spmd.clone, body=%wide.region_4.7_spmd.clone.sunk | while | flops 16812052 | bytes 590521 | solution.py:66
  44.2 4.1 %fusion.50 = (f32[]{:T(128)}, f32[]{:T(128)}) fusion(f32[]{:T(128)} %bitcast.119, f32[16,128]{1,0:T(8,128)S(1)} %get-tuple-element.546, f32[16,128]{1,0:T(8,128)S(1)} %get-tuple-element.547, f32[16,128]{1,0:T(8,128)S(1)} %get-tuple-element.548, f32[16,128]{1,0:T(8,128)S(1)} %get-tuple-element.549, f32[16,128]{1,0:T(8,128)S(1)} %get-tuple-element.550, ...), kind=kLoop, calls=%fused_computation.20.clone.1 | loop fusion | flops 9699326 | bytes 163928 | tf_op jit(solution)/shard_map/while/body/eval_jaxpr/while/body/eval_jaxpr/reduce_sum | solution.py:52
  49.5 3.4 %fusion.51 = f32[]{:T(128)} fusion(f32[]{:T(128)} %bitcast.121, f32[]{:T(128)} %get-tuple-element.604, f32[16,128]{1,0:T(8,128)S(1)} %get-tuple-element.546, f32[16,128]{1,0:T(8,128)S(1)} %get-tuple-element.547, f32[16,128]{1,0:T(8,128)S(1)} %get-tuple-element.548, f32[16,128]{1,0:T(8,128)S(1)} %get-tuple-element.549, ...), kind=kLoop, calls=%fused_computation.23.clone.1 | loop fusion | flops 7077887 | bytes 163916 | tf_op jit(solution)/shard_map/while/body/eval_jaxpr/while/body/eval_jaxpr/reduce_sum | solution.py:52
  56.3 4.1 %fusion.50 = (f32[]{:T(128)}, f32[]{:T(128)}) fusion(f32[]{:T(128)} %bitcast.119, f32[16,128]{1,0:T(8,128)S(1)} %get-tuple-element.546, f32[16,128]{1,0:T(8,128)S(1)} %get-tuple-element.547, f32[16,128]{1,0:T(8,128)S(1)} %get-tuple-element.548, f32[16,128]{1,0:T(8,128)S(1)} %get-tuple-element.549, f32[16,128]{1,0:T(8,128)S(1)} %get-tuple-element.550, ...), kind=kLoop, calls=%fused_computation.20.clone.1 | loop fusion | flops 9699326 | bytes 163928 | tf_op jit(solution)/shard_map/while/body/eval_jaxpr/while/body/eval_jaxpr/reduce_sum | solution.py:52
  61.6 3.4 %fusion.51 = f32[]{:T(128)} fusion(f32[]{:T(128)} %bitcast.121, f32[]{:T(128)} %get-tuple-element.604, f32[16,128]{1,0:T(8,128)S(1)} %get-tuple-element.546, f32[16,128]{1,0:T(8,128)S(1)} %get-tuple-element.547, f32[16,128]{1,0:T(8,128)S(1)} %get-tuple-element.548, f32[16,128]{1,0:T(8,128)S(1)} %get-tuple-element.549, ...), kind=kLoop, calls=%fused_computation.23.clone.1 | loop fusion | flops 7077887 | bytes 163916 | tf_op jit(solution)/shard_map/while/body/eval_jaxpr/while/body/eval_jaxpr/reduce_sum | solution.py:52
  68.4 4.1 %fusion.50 = (f32[]{:T(128)}, f32[]{:T(128)}) fusion(f32[]{:T(128)} %bitcast.119, f32[16,128]{1,0:T(8,128)S(1)} %get-tuple-element.546, f32[16,128]{1,0:T(8,128)S(1)} %get-tuple-element.547, f32[16,128]{1,0:T(8,128)S(1)} %get-tuple-element.548, f32[16,128]{1,0:T(8,128)S(1)} %get-tuple-element.549, f32[16,128]{1,0:T(8,128)S(1)} %get-tuple-element.550, ...), kind=kLoop, calls=%fused_computation.20.clone.1 | loop fusion | flops 9699326 | bytes 163928 | tf_op jit(solution)/shard_map/while/body/eval_jaxpr/while/body/eval_jaxpr/reduce_sum | solution.py:52
  73.7 3.4 %fusion.51 = f32[]{:T(128)} fusion(f32[]{:T(128)} %bitcast.121, f32[]{:T(128)} %get-tuple-element.604, f32[16,128]{1,0:T(8,128)S(1)} %get-tuple-element.546, f32[16,128]{1,0:T(8,128)S(1)} %get-tuple-element.547, f32[16,128]{1,0:T(8,128)S(1)} %get-tuple-element.548, f32[16,128]{1,0:T(8,128)S(1)} %get-tuple-element.549, ...), kind=kLoop, calls=%fused_computation.23.clone.1 | loop fusion | flops 7077887 | bytes 163916 | tf_op jit(solution)/shard_map/while/body/eval_jaxpr/while/body/eval_jaxpr/reduce_sum | solution.py:52
  80.5 4.1 %fusion.50 = (f32[]{:T(128)}, f32[]{:T(128)}) fusion(f32[]{:T(128)} %bitcast.119, f32[16,128]{1,0:T(8,128)S(1)} %get-tuple-element.546, f32[16,128]{1,0:T(8,128)S(1)} %get-tuple-element.547, f32[16,128]{1,0:T(8,128)S(1)} %get-tuple-element.548, f32[16,128]{1,0:T(8,128)S(1)} %get-tuple-element.549, f32[16,128]{1,0:T(8,128)S(1)} %get-tuple-element.550, ...), kind=kLoop, calls=%fused_computation.20.clone.1 | loop fusion | flops 9699326 | bytes 163928 | tf_op jit(solution)/shard_map/while/body/eval_jaxpr/while/body/eval_jaxpr/reduce_sum | solution.py:52
  85.8 3.4 %fusion.51 = f32[]{:T(128)} fusion(f32[]{:T(128)} %bitcast.121, f32[]{:T(128)} %get-tuple-element.604, f32[16,128]{1,0:T(8,128)S(1)} %get-tuple-element.546, f32[16,128]{1,0:T(8,128)S(1)} %get-tuple-element.547, f32[16,128]{1,0:T(8,128)S(1)} %get-tuple-element.548, f32[16,128]{1,0:T(8,128)S(1)} %get-tuple-element.549, ...), kind=kLoop, calls=%fused_computation.23.clone.1 | loop fusion | flops 7077887 | bytes 163916 | tf_op jit(solution)/shard_map/while/body/eval_jaxpr/while/body/eval_jaxpr/reduce_sum | solution.py:52
  94.6 48.4 %while.39 = (s32[]{:T(128)}, f32[3]{0:T(128)S(1)}, f32[3]{0:T(128)S(1)}, f32[64]{0:T(128)S(1)}, f32[6,64,128]{2,1,0:T(8,128)S(1)}, /*index=5*/f32[6,64,128]{2,1,...) while((s32[]{:T(128)}, f32[3]{0:T(128)S(1)}, ...), condition=%wide.region_8.8_spmd.clone, body=%wide.region_4.7_spmd.clone.sunk | while | flops 16812052 | bytes 590521 | solution.py:66
  95.4 4.1 %fusion.50 = (f32[]{:T(128)}, f32[]{:T(128)}) fusion(f32[]{:T(128)} %bitcast.119, f32[16,128]{1,0:T(8,128)S(1)} %get-tuple-element.546, f32[16,128]{1,0:T(8,128)S(1)} %get-tuple-element.547, f32[16,128]{1,0:T(8,128)S(1)} %get-tuple-element.548, f32[16,128]{1,0:T(8,128)S(1)} %get-tuple-element.549, f32[16,128]{1,0:T(8,128)S(1)} %get-tuple-element.550, ...), kind=kLoop, calls=%fused_computation.20.clone.1 | loop fusion | flops 9699326 | bytes 163928 | tf_op jit(solution)/shard_map/while/body/eval_jaxpr/while/body/eval_jaxpr/reduce_sum | solution.py:52
  100.7 3.4 %fusion.51 = f32[]{:T(128)} fusion(f32[]{:T(128)} %bitcast.121, f32[]{:T(128)} %get-tuple-element.604, f32[16,128]{1,0:T(8,128)S(1)} %get-tuple-element.546, f32[16,128]{1,0:T(8,128)S(1)} %get-tuple-element.547, f32[16,128]{1,0:T(8,128)S(1)} %get-tuple-element.548, f32[16,128]{1,0:T(8,128)S(1)} %get-tuple-element.549, ...), kind=kLoop, calls=%fused_computation.23.clone.1 | loop fusion | flops 7077887 | bytes 163916 | tf_op jit(solution)/shard_map/while/body/eval_jaxpr/while/body/eval_jaxpr/reduce_sum | solution.py:52
  107.5 4.1 %fusion.50 = (f32[]{:T(128)}, f32[]{:T(128)}) fusion(f32[]{:T(128)} %bitcast.119, f32[16,128]{1,0:T(8,128)S(1)} %get-tuple-element.546, f32[16,128]{1,0:T(8,128)S(1)} %get-tuple-element.547, f32[16,128]{1,0:T(8,128)S(1)} %get-tuple-element.548, f32[16,128]{1,0:T(8,128)S(1)} %get-tuple-element.549, f32[16,128]{1,0:T(8,128)S(1)} %get-tuple-element.550, ...), kind=kLoop, calls=%fused_computation.20.clone.1 | loop fusion | flops 9699326 | bytes 163928 | tf_op jit(solution)/shard_map/while/body/eval_jaxpr/while/body/eval_jaxpr/reduce_sum | solution.py:52
  112.8 3.4 %fusion.51 = f32[]{:T(128)} fusion(f32[]{:T(128)} %bitcast.121, f32[]{:T(128)} %get-tuple-element.604, f32[16,128]{1,0:T(8,128)S(1)} %get-tuple-element.546, f32[16,128]{1,0:T(8,128)S(1)} %get-tuple-element.547, f32[16,128]{1,0:T(8,128)S(1)} %get-tuple-element.548, f32[16,128]{1,0:T(8,128)S(1)} %get-tuple-element.549, ...), kind=kLoop, calls=%fused_computation.23.clone.1 | loop fusion | flops 7077887 | bytes 163916 | tf_op jit(solution)/shard_map/while/body/eval_jaxpr/while/body/eval_jaxpr/reduce_sum | solution.py:52
  119.6 4.1 %fusion.50 = (f32[]{:T(128)}, f32[]{:T(128)}) fusion(f32[]{:T(128)} %bitcast.119, f32[16,128]{1,0:T(8,128)S(1)} %get-tuple-element.546, f32[16,128]{1,0:T(8,128)S(1)} %get-tuple-element.547, f32[16,128]{1,0:T(8,128)S(1)} %get-tuple-element.548, f32[16,128]{1,0:T(8,128)S(1)} %get-tuple-element.549, f32[16,128]{1,0:T(8,128)S(1)} %get-tuple-element.550, ...), kind=kLoop, calls=%fused_computation.20.clone.1 | loop fusion | flops 9699326 | bytes 163928 | tf_op jit(solution)/shard_map/while/body/eval_jaxpr/while/body/eval_jaxpr/reduce_sum | solution.py:52
  124.9 3.4 %fusion.51 = f32[]{:T(128)} fusion(f32[]{:T(128)} %bitcast.121, f32[]{:T(128)} %get-tuple-element.604, f32[16,128]{1,0:T(8,128)S(1)} %get-tuple-element.546, f32[16,128]{1,0:T(8,128)S(1)} %get-tuple-element.547, f32[16,128]{1,0:T(8,128)S(1)} %get-tuple-element.548, f32[16,128]{1,0:T(8,128)S(1)} %get-tuple-element.549, ...), kind=kLoop, calls=%fused_computation.23.clone.1 | loop fusion | flops 7077887 | bytes 163916 | tf_op jit(solution)/shard_map/while/body/eval_jaxpr/while/body/eval_jaxpr/reduce_sum | solution.py:52
  131.7 4.1 %fusion.50 = (f32[]{:T(128)}, f32[]{:T(128)}) fusion(f32[]{:T(128)} %bitcast.119, f32[16,128]{1,0:T(8,128)S(1)} %get-tuple-element.546, f32[16,128]{1,0:T(8,128)S(1)} %get-tuple-element.547, f32[16,128]{1,0:T(8,128)S(1)} %get-tuple-element.548, f32[16,128]{1,0:T(8,128)S(1)} %get-tuple-element.549, f32[16,128]{1,0:T(8,128)S(1)} %get-tuple-element.550, ...), kind=kLoop, calls=%fused_computation.20.clone.1 | loop fusion | flops 9699326 | bytes 163928 | tf_op jit(solution)/shard_map/while/body/eval_jaxpr/while/body/eval_jaxpr/reduce_sum | solution.py:52
  143.0 38.9 %psum.7 = f32[2,3]{1,0:T(2,128)S(1)} all-reduce(f32[2,3]{1,0:T(2,128)S(1)} %get-tuple-element.224), channel_id=1, replica_groups=mesh['win'=2,'grp'=16] {'grp'}, use_global_device_ids=true, to_apply=%region_10.11 | all-reduce | flops 6 | bytes 48 | tf_op jit(solution)/shard_map/psum | solution.py:129
  186.5 4.1 %collective-permute-start.1 = (f32[1]{0:T(128)}, f32[1]{0:T(128)}, u32[]{:S(2)}, u32[]{:S(2)}) collective-permute-start(f32[1]{0:T(128)} %bitcast.30), channel_id=1, source_target_pairs={{0,16},{1,17},{2,18},{3,19},{4,20},{5,21},{6,22},{7,23},{8,24},{9,... | collective-permute-start | bytes 20 | tf_op jit(solution)/shard_map/ppermute | solution.py:15
  (131 shorter events, 35.4 us)
Async XLA Ops:
  0.6 26.4 %copy-start = (f32[4]{0:T(128)S(1)}, f32[4]{0:T(128)}, u32[]{:S(2)}) copy-start(f32[4]{0:T(128)} %param.16) | copy-start | bytes 52
  1.8 10.7 %copy-start.2 = (f32[2,6,1536]{2,0,1:T(2,128)S(1)}, f32[2,6,1536]{2,0,1:T(2,128)}, u32[]{:S(2)}) copy-start(f32[2,6,1536]{2,0,1:T(2,128)} %param.13) | copy-start | bytes 221188
  2.8 15.7 %all-to-all-start = ((s32[2,16,5]{2,0,1:T(2,128)}), s32[2,16,5]{2,0,1:T(2,128)S(1)}, u32[]{:S(2)}, u32[]{:S(2)}) async-start(s32[2,16,5]{2,0,1:T(2,128)} %copy.51), calls=%async_computation | async-start | bytes 32768 | tf_op jit(solution)/shard_map/all_to_all | solution.py:105
  11.8 0.7 copy-start.5
  22.2 16.9 %all-to-all-start.1 = ((f32[2,6,16,5,128]{4,0,3,1,2:T(2,128)}), f32[2,6,16,5,128]{4,0,3,1,2:T(2,128)S(1)}, u32[]{:S(2)}, u32[]{:S(2)}) async-start(f32[2,6,16,5,128]{4,0,3,1,2:T(2,128)} %copy.58), calls=%async_computation.1 | async-start | bytes 983040 | tf_op jit(solution)/shard_map/all_to_all | solution.py:112
  28.3 2.1 %copy-start.1 = (s32[4]{0:T(128)S(1)}, s32[4]{0:T(128)}, u32[]{:S(2)}) copy-start(s32[4]{0:T(128)} %param.19) | copy-start | bytes 52
  29.1 0.7 copy-start.6
  31.1 0.7 copy-start.4
  181.9 0.7 copy-start.3
  183.2 9.9 %collective-permute-start = (f32[1]{0:T(128)}, f32[1]{0:T(128)}, u32[]{:S(2)}, u32[]{:S(2)}) collective-permute-start(f32[1]{0:T(128)} %bitcast.29), channel_id=1, source_target_pairs={{16,0},{17,1},{18,2},{19,3},{20,4},{21,5},{22,6},{23,7},{24,8},{25... | collective-permute-start | bytes 20 | tf_op jit(solution)/shard_map/ppermute | solution.py:15
  186.5 6.7 %collective-permute-start.1 = (f32[1]{0:T(128)}, f32[1]{0:T(128)}, u32[]{:S(2)}, u32[]{:S(2)}) collective-permute-start(f32[1]{0:T(128)} %bitcast.30), channel_id=1, source_target_pairs={{0,16},{1,17},{2,18},{3,19},{4,20},{5,21},{6,22},{7,23},{8,24},{9,... | collective-permute-start | bytes 20 | tf_op jit(solution)/shard_map/ppermute | solution.py:15
where the time goes:
time: 198 us; the launch traced here: 196 us
  other arithmetic  66.4 us (34%)
  blocking collectives  41.3 us (21%)
  loops' own time  34.5 us (17%)
  local copies, waits for them, and re-layouts  21.4 us (11%)
  starting transfers between devices  17.3 us (9%)
  waiting for transfers between devices  13.1 us (7%)
  between operations  2.22 us (1%)
    reduce_sum x16, other arithmetic, pair_energy(): totals.append(lam_now * jnp.sum(keep_mask * (dispersion + coulomb)))  59.4 us
    psum x1, blocking collectives, per_device(): summed = lax.psum(partial_sums, 'grp')  38.9 us
    another operation x2, loops' own time, evaluate(): return lax.fori_loop(0, count, advance, jnp.zeros((3,), jnp.float32))  30.6 us
    all_to_all x1, starting transfers between devices, per_device(): lax.all_to_all(requests, 'grp', split_axis=1, concat_axis=1, tiled=True)  8.34 us
    all_to_all x1, waiting for transfers between devices, per_device(): lax.all_to_all(replies, 'grp', split_axis=2, concat_axis=2, tiled=True)  7.31 us
    slice x10, local copies, waits for them, and re-layouts, pair_energy(): lam_now = lambda_set[number]  6.66 us
    all_to_all x1, waiting for transfers between devices, per_device(): lax.all_to_all(requests, 'grp', split_axis=1, concat_axis=1, tiled=True)  5.81 us
    ppermute x2, starting transfers between devices, from_behind(): return lax.ppermute(shard, axis, pairs)  5.36 us
  transfers between devices with their start and end apart: 4, of which 2 were waited for; matrix products, arithmetic and copies ran while one was open for 3% of the time, Pallas kernels for 0%

commit v1 on v0

v1 whole, which is shorter than its diff:
```python
import functools

import jax
import jax.numpy as jnp
from jax import lax
from jax.experimental import pallas as pl
from jax.experimental.pallas import tpu as pltpu
from jax.sharding import PartitionSpec as P

TILE = 128
ROWS = 8
FIELDS = 6
PIECES = TILE // ROWS
MESH = pl.DeviceIdType.MESH


def grid_of(mesh):
    groups = mesh.shape["grp"]
    try:
        line = mesh.devices[0]
        coords = [tuple(d.coords) for d in line]
        dims = [len({c[a] for c in coords}) for a in (2, 1, 0)]
        base = [min(c[a] for c in coords) for a in (2, 1, 0)]
        want = [
            (base[2] + x, base[1] + y, base[0] + z)
            for z in range(dims[0])
            for y in range(dims[1])
            for x in range(dims[2])
        ]
        if [c[:3] for c in coords] == want:
            return tuple(dims)
    except Exception:
        pass
    return (groups, 1, 1)


def messages_of(dims):
    z, y, x = dims
    first = (z - 1) + (x - 1) + (y - 1)
    second = (z - 1) * (x + y - 2)
    third = z * (x - 1) * (y - 1)
    return first + second + third


def kernel(
    cfg,
    table,
    row_ids,
    col_ids,
    lambdas,
    inverse_temp,
    parity,
    thresholds,
    out_energy,
    out_margin,
    out_profile,
    *scratch,
):
    run, wins, groups, own, listed, dims = cfg
    bufs = scratch[:run]
    rowbs = scratch[run : 2 * run]
    red, send_sem, recv_sem, red_send, red_recv = scratch[2 * run :]
    dim_z, dim_y, dim_x = dims
    devices = wins * groups
    windows = wins * run
    win = lax.axis_index("win")
    grp = lax.axis_index("grp")
    me = win * groups + grp
    my_z = grp // (dim_y * dim_x)
    my_y = (grp // dim_x) % dim_y
    my_x = grp % dim_x
    two_ends = wins == 2 and run == 2

    def window_of(slot):
        if two_ends:
            return jnp.where(win == 0, slot, 1 - slot)
        return slot

    def at(dz, dy, dx):
        return (
            ((my_z + dz) % dim_z) * dim_y + (my_y + dy) % dim_y
        ) * dim_x + (my_x + dx) % dim_x

    barrier = pltpu.get_barrier_semaphore()

    def greet(step, carry):
        other = (me + step) % devices
        pl.semaphore_signal(
            barrier, inc=1, device_id=(other // groups, other % groups), device_id_type=MESH
        )
        return carry

    lax.fori_loop(1, devices, greet, 0)

    def spread(slot):
        local = window_of(slot)

        def one(block, carry):
            start = pl.multiple_of(block * TILE, TILE)
            tile = table[local, :, pl.ds(start, TILE)]
            packed = jnp.concatenate(
                [tile[0:4], 4.0 * tile[4:5], 1.0 / tile[5:6], tile[0:2]], axis=0
            )
            turned = jnp.transpose(packed)
            for field in range(FIELDS):
                wide = jnp.broadcast_to(turned[:, field : field + 1], (TILE, TILE))
                for piece in range(PIECES):
                    rowbs[slot][(block * FIELDS + field) * PIECES + piece] = wide[
                        piece * ROWS : (piece + 1) * ROWS
                    ]
            bufs[slot][grp * own + block] = tile
            return carry

        lax.fori_loop(0, own, one, 0)

    spread(0)

    shares = []
    lowers = []
    for wl in range(run):
        window = win * run + wl
        odd = (window + parity[0]) & 1
        lower = window - odd
        threshold = thresholds[0]
        for v in range(1, windows):
            threshold = jnp.where(lower == v, thresholds[v], threshold)
        drawn = ((threshold + parity[0]) & 1073741823) + 1
        share = jnp.full((ROWS, TILE), drawn, jnp.int32).astype(jnp.float32) * (1.0 / 1073741824.0)
        shares.append(-jnp.log(share))
        lowers.append(lower)

    pl.semaphore_wait(barrier, devices - 1)

    counts = [0] * run

    def share_of(slot, owner):
        return bufs[slot].at[pl.ds(owner * own, own)]

    def descriptor(slot, owner, target, number):
        return pltpu.make_async_remote_copy(
            src_ref=share_of(slot, owner),
            dst_ref=share_of(slot, owner),
            send_sem=send_sem.at[slot, number],
            recv_sem=recv_sem.at[slot, owner],
            device_id={"grp": target},
            device_id_type=MESH,
        )

    sent = []

    def send(slot, owner, target):
        copy = descriptor(slot, owner, target, counts[slot])
        counts[slot] += 1
        copy.start()
        sent.append(copy)

    def arrived(slot, owner):
        descriptor(slot, owner, owner, 0).wait_recv()

    def to_x(slot, owner):
        for dx in range(1, dim_x):
            send(slot, owner, at(0, 0, dx))

    def to_y(slot, owner):
        for dy in range(1, dim_y):
            send(slot, owner, at(0, dy, 0))

    def open_sends(slot):
        for dz in range(1, dim_z):
            send(slot, grp, at(dz, 0, 0))
        to_x(slot, grp)
        to_y(slot, grp)

    def pass_plane(slot, dz):
        for dx in range(1, dim_x):
            owner = at(dz, 0, dx)
            arrived(slot, owner)
            if dz % 2 == 0:
                to_y(slot, owner)
        for dy in range(1, dim_y):
            owner = at(dz, dy, 0)
            arrived(slot, owner)
            if dz % 2 == 1:
                to_x(slot, owner)

    def pass_column(slot):
        for dz in range(1, dim_z):
            owner = at(dz, 0, 0)
            arrived(slot, owner)
            to_x(slot, owner)
            to_y(slot, owner)

    def pass_planes(slot):
        for dz in range(dim_z):
            pass_plane(slot, dz)

    def last_arrivals(slot):
        for dz in range(dim_z):
            for dy in range(1, dim_y):
                for dx in range(1, dim_x):
                    arrived(slot, at(dz, dy, dx))

    def lambda_list(slot):
        window = win * run + window_of(slot)
        if two_ends and slot == 0:
            low = jnp.where(window == 0, 0, window - 1)
            return [lambdas[low], lambdas[low + 1]]
        return [
            lambdas[jnp.maximum(window - 1, 0)],
            lambdas[window],
            lambdas[jnp.minimum(window + 1, windows - 1)],
        ]

    def start_state(slot):
        zero = jnp.zeros((ROWS, TILE), jnp.float32)
        row = jnp.zeros((1, TILE), jnp.float32)
        return tuple(zero for _ in lambda_list(slot)) + (row, row)

    def tiles(slot, first, last, state):
        local = window_of(slot)
        lams = lambda_list(slot)
        cores = [1.0 - 0.5 * lam for lam in lams]
        softs = [2.0 - lam for lam in lams]
        base = grp * own

        def one(pair, state):
            row_id = row_ids[local, pair]
            col_id = col_ids[local, pair]
            col = bufs[slot][col_id]
            mine = jnp.clip(row_id - base, 0, own - 1) * (FIELDS * PIECES)
            fields = [jnp.broadcast_to(col[f : f + 1], (ROWS, TILE)) for f in range(3)]
            charge_col = col[3:4]
            depth_col = col[4:5]
            size_col = jnp.broadcast_to(1.0 / col[5:6], (ROWS, TILE))
            sum_disp = [None] * len(lams)
            sum_coul = [None] * len(lams)
            for piece in range(TILE // ROWS):
                dx = rowbs[slot][mine + piece] - fields[0]
                dy = rowbs[slot][mine + 1 * PIECES + piece] - fields[1]
                dz = rowbs[slot][mine + 2 * PIECES + piece] - fields[2]
                charge = rowbs[slot][mine + 3 * PIECES + piece]
                depth = rowbs[slot][mine + 4 * PIECES + piece]
                r2 = dx * dx + dy * dy + dz * dz
                scaled = r2 * (rowbs[slot][mine + 5 * PIECES + piece] * size_col)
                cube = scaled * scaled * scaled
                for k in range(len(lams)):
                    root = lax.rsqrt(cube + cores[k])
                    inverse = root * root
                    disp = (depth * inverse) * (inverse - 1.0)
                    coul = charge * lax.rsqrt(r2 + softs[k])
                    if piece == 0:
                        sum_disp[k], sum_coul[k] = disp, coul
                    else:
                        sum_disp[k] = sum_disp[k] + disp
                        sum_coul[k] = sum_coul[k] + coul
            totals = [
                state[k] + (sum_disp[k] * depth_col + sum_coul[k] * charge_col)
                for k in range(len(lams))
            ]
            same = jnp.where(row_id == col_id, 1.0, 0.0)
            return tuple(totals) + (
                state[-2] + same * (depth_col * depth_col),
                state[-1] + same * (charge_col * charge_col),
            )

        return lax.fori_loop(first, last, one, state)

    def close(slot, state):
        out = []
        for k, lam in enumerate(lambda_list(slot)):
            core = jnp.full((1, TILE), 1.0 - 0.5 * lam, jnp.float32)
            soft = jnp.full((1, TILE), 2.0 - lam, jnp.float32)
            inverse = 1.0 / core
            own_pairs = state[-2] * (4.0 * inverse * (inverse - 1.0)) + state[-1] * lax.rsqrt(soft)
            line = jnp.sum(state[k], axis=0, keepdims=True) - own_pairs
            out.append(jnp.sum(line, axis=1, keepdims=True) * lam)
        if two_ends and slot == 0:
            out = [out[0], jnp.where(win == 0, out[0], out[1]), out[1]]
        return out

    open_sends(0)
    for slot in range(1, run):
        spread(slot)
        open_sends(slot)
    pass_column(0)
    if run > 1:
        pass_column(1)
    pass_planes(0)
    last_arrivals(0)
    partial = []
    for slot in range(run):
        state = start_state(slot)
        if slot + 1 < run:
            half = (3 * listed) // 8
            state = tiles(slot, 0, half, state)
            if slot > 0:
                pass_column(slot + 1)
            pass_planes(slot + 1)
            state = tiles(slot, half, listed, state)
            last_arrivals(slot + 1)
        else:
            state = tiles(slot, 0, listed, state)
        partial.append(close(slot, state))

    lane = lax.broadcasted_iota(jnp.int32, (1, TILE), 1)
    line = jnp.zeros((1, TILE), jnp.float32)
    for slot in range(run):
        place = window_of(slot) * 3
        for k in range(3):
            line = jnp.where(lane == place + k, partial[slot][k], line)
    red[me] = line

    def share_out(step, carry):
        other = (me + step) % devices
        pltpu.make_async_remote_copy(
            src_ref=red.at[me],
            dst_ref=red.at[me],
            send_sem=red_send.at[step],
            recv_sem=red_recv.at[me],
            device_id=(other // groups, other % groups),
            device_id_type=MESH,
        ).start()
        return carry

    lax.fori_loop(1, devices, share_out, 0)
    for copy in sent:
        copy.wait_send()

    def collect(step, carry):
        other = (me + step) % devices
        copy = pltpu.make_async_remote_copy(
            src_ref=red.at[other],
            dst_ref=red.at[other],
            send_sem=red_send.at[step],
            recv_sem=red_recv.at[other],
            device_id=(other // groups, other % groups),
            device_id_type=MESH,
        )
        copy.wait_recv()
        copy.wait_send()
        return carry

    lax.fori_loop(1, devices, collect, 0)
    scale = 1.0 / (listed * groups * TILE * TILE)
    energy = []
    for part in range(wins):
        total = jnp.sum(red[part * groups : (part + 1) * groups], axis=0) * scale
        for wl in range(run):
            energy.append(
                [jnp.sum(jnp.where(lane == wl * 3 + k, total, 0.0)) for k in range(3)]
            )
    ups = [e[2] - e[1] for e in energy]
    downs = [e[0] - e[1] for e in energy]
    for wl in range(run):
        window = win * run + wl
        for k in range(3):
            value = energy[wl][k]
            for part in range(1, wins):
                value = jnp.where(win == part, energy[part * run + wl][k], value)
            out_energy[wl, k] = value
        profile = jnp.float32(0.0)
        change = jnp.float32(0.0)
        for v in range(windows):
            profile = profile + jnp.where(v < window, ups[v], 0.0)
            change = change + jnp.where(lowers[wl] == v, ups[v], 0.0)
            change = change + jnp.where(lowers[wl] + 1 == v, downs[v], 0.0)
        out_profile[wl] = profile
        partner = jnp.logical_and(lowers[wl] >= 0, lowers[wl] + 1 < windows)
        margin = jnp.max(shares[wl]) - inverse_temp[0] * change
        out_margin[wl] = jnp.where(partner, margin, 0.0)


def per_device(dims, atom_table, row_blocks, col_blocks, lambdas, inverse_temp, parity, thresholds):
    run, fields, atoms = atom_table.shape
    wins = lax.axis_size("win")
    groups = lax.axis_size("grp")
    own = atoms // TILE
    listed = row_blocks.shape[1]
    cfg = (run, wins, groups, own, listed, dims)
    smem = pl.BlockSpec(memory_space=pltpu.SMEM)
    vmem = pl.BlockSpec(memory_space=pltpu.VMEM)
    devices = wins * groups
    scratch = [pltpu.VMEM((groups * own, fields, TILE), jnp.float32) for _ in range(run)]
    scratch += [pltpu.VMEM((own * FIELDS * PIECES, ROWS, TILE), jnp.float32) for _ in range(run)]
    scratch += [
        pltpu.VMEM((devices, 1, TILE), jnp.float32),
        pltpu.SemaphoreType.DMA((run, max(1, messages_of(dims)))),
        pltpu.SemaphoreType.DMA((run, groups)),
        pltpu.SemaphoreType.DMA((devices,)),
        pltpu.SemaphoreType.DMA((devices,)),
    ]
    return pl.pallas_call(
        functools.partial(kernel, cfg),
        out_shape=(
            jax.ShapeDtypeStruct((run, 3), jnp.float32),
            jax.ShapeDtypeStruct((run,), jnp.float32),
            jax.ShapeDtypeStruct((run,), jnp.float32),
        ),
        in_specs=[vmem, smem, smem, smem, smem, smem, smem],
        out_specs=(smem, smem, smem),
        scratch_shapes=scratch,
        compiler_params=pltpu.CompilerParams(
            collective_id=0, has_side_effects=True, vmem_limit_bytes=48 * 1024 * 1024
        ),
    )(atom_table, row_blocks, col_blocks, lambdas, inverse_temp, parity, thresholds)


def solution(mesh):
    return jax.shard_map(
        functools.partial(per_device, grid_of(mesh)),
        mesh=mesh,
        in_specs=(P("win", None, "grp"), P("win", "grp"), P("win", "grp"), P(), P(), P(), P()),
        out_specs=(P("win", None), P("win"), P("win")),
        check_vma=False,
    )
```

time: 198 us -> 46.9 us (0.24)
  other arithmetic: 66.4 us -> 0 us
  Pallas kernels: 0 us -> 42.2 us
  blocking collectives: 41.3 us -> 0 us
  loops' own time: 34.5 us -> 0 us
  local copies, waits for them, and re-layouts: 21.4 us -> 2.53 us
  starting transfers between devices: 17.3 us -> 0 us
  waiting for transfers between devices: 13.1 us -> 0 us
    reduce_sum x18 -> x0, other arithmetic: 59.9 us -> none  [the longest x16 59.4 us: pair_energy(): totals.append(lam_now * jnp.sum(keep_mask * (dispersion + coulomb)))]
    pallas_call x0 -> x1, Pallas kernels: none -> 42.2 us  [per_device(): pl.pallas_call(functools.partial(kernel, cfg), out_shape=(jax.ShapeDtypeS...]
    psum x1 -> x0, blocking collectives: 38.9 us -> none  [per_device(): summed = lax.psum(partial_sums, 'grp')]
    another operation x4 -> x0, loops' own time: 34.5 us -> none  [the longest x2 30.6 us: evaluate(): return lax.fori_loop(0, count, advance, jnp.zeros((3,), jnp.float32))]
    all_to_all x2 -> x0, waiting for transfers between devices: 13.1 us -> none  [the longest x1 7.31 us: per_device(): lax.all_to_all(replies, 'grp', split_axis=2, concat_axis=2, tiled=True)]
    all_to_all x2 -> x0, starting transfers between devices: 11.9 us -> none  [the longest x1 8.34 us: per_device(): lax.all_to_all(requests, 'grp', split_axis=1, concat_axis=1, tiled=True)]
    slice x12 -> x0, local copies, waits for them, and re-layouts: 7.8 us -> none  [the longest x10 6.66 us: pair_energy(): lam_now = lambda_set[number]]
    gather x13 -> x0, local copies, waits for them, and re-layouts: 6.6 us -> none  [the longest x6 2.35 us: take_blocks(): return jnp.take(source, indices, axis=1)]
  transfers between devices with their start and end apart: 4 -> 0, of which waited for: 2 -> 0; matrix products, arithmetic and copies ran while one was open for 3% -> 0% of each run, Pallas kernels for 0% -> 0%
where the time goes in v1:
time: 46.9 us; the launch traced here: 46.7 us
  Pallas kernels  42.2 us (90%)
  local copies, waits for them, and re-layouts  2.53 us (5%)
  between operations  2 us (4%)
    pallas_call x1, Pallas kernels, per_device(): pl.pallas_call(functools.partial(kernel, cfg), out_shape=(jax.ShapeDtypeS...  42.2 us
    unnamed x12, local copies, waits for them, and re-layouts  2.53 us

profile of v1, /device:TPU:0, one launch (start us, length us, event | category | flops | bytes accessed | tf_op | source)
XLA Modules:
  0.0 46.7 jit_solution(6837378804596614780)
XLA Ops:
  1.9 0.0 copy-start
  1.9 0.0 copy-start.1
  1.9 0.0 copy-start.2
  2.0 0.0 copy-start.3
  2.0 0.9 %copy.10.table = f32[2,6,1536]{2,1,0:T(8,128)S(1)} copy(f32[2,6,1536]{2,0,1:T(2,128)} %param.7) | data formatting | bytes 147456 | tf_op args[0]
  2.9 0.0 copy-done
  2.9 0.0 copy-done.1
  2.9 0.0 copy-done.2
  2.9 0.0 copy-done.3
  2.9 42.2 %shard_map.94 = (f32[2,3]{1,0:T(2,128)S(1)}, f32[2]{0:T(128)S(1)}, f32[2]{0:T(128)S(1)}) custom-call(f32[2,6,1536]{2,1,0:T(8,128)S(1)} %copy.10.table, s32[2,64]{1,0:T(2,128)S(1)} %copy-done, s32[2,64]{1,0:T(2,128)S(1)} %copy-done.1, f32[4]{0:T(128)S(1)} %copy-done.2, f32[1]{0:T(128)S(6)} %copy.14.inverse_temp, s32[1]{0:T(128)S(6)} %copy.15.parity, ...), custom_call_target="tpu_custom_call" | custom-call | tf_op jit(solution)/shard_map/pallas_call | solution.py:392
  45.1 0.6 %copy.16 = f32[2,3]{1,0:T(2,128)} copy(f32[2,3]{1,0:T(2,128)S(1)} %get-tuple-element.6) | data formatting | bytes 48
  45.7 0.5 %copy.17 = f32[2]{0:T(128)} copy(f32[2]{0:T(128)S(1)} %get-tuple-element.7) | data formatting | bytes 16
  46.2 0.5 %copy.18 = f32[2]{0:T(128)} copy(f32[2]{0:T(128)S(1)} %get-tuple-element.8) | data formatting | bytes 16
Async XLA Ops:
  1.9 1.0 %copy-start = (s32[2,64]{1,0:T(2,128)S(1)}, s32[2,64]{1,0:T(2,128)}, u32[]{:S(2)}) copy-start(s32[2,64]{1,0:T(2,128)} %row_ids.1) | copy-start | bytes 1540
  1.9 1.0 %copy-start.1 = (s32[2,64]{1,0:T(2,128)S(1)}, s32[2,64]{1,0:T(2,128)}, u32[]{:S(2)}) copy-start(s32[2,64]{1,0:T(2,128)} %col_ids.1) | copy-start | bytes 1540
  1.9 1.0 %copy-start.2 = (f32[4]{0:T(128)S(1)}, f32[4]{0:T(128)}, u32[]{:S(2)}) copy-start(f32[4]{0:T(128)} %lambdas.1) | copy-start | bytes 52
  2.0 1.0 %copy-start.3 = (s32[4]{0:T(128)S(1)}, s32[4]{0:T(128)}, u32[]{:S(2)}) copy-start(s32[4]{0:T(128)} %thresholds.1) | copy-start | bytes 52

commit v2 on v1

--- a/solution.py
+++ b/solution.py
@@ -73,7 +73,7 @@
 
     def window_of(slot):
         if two_ends:
-            return jnp.where(win == 0, slot, 1 - slot)
+            return jnp.where(win == 0, 1 - slot, slot)
         return slot
 
     def at(dz, dy, dx):
@@ -108,12 +108,19 @@
                     rowbs[slot][(block * FIELDS + field) * PIECES + piece] = wide[
                         piece * ROWS : (piece + 1) * ROWS
                     ]
-            bufs[slot][grp * own + block] = tile
             return carry
 
         lax.fori_loop(0, own, one, 0)
 
-    spread(0)
+    def pack(block, carry):
+        start = pl.multiple_of(block * TILE, TILE)
+        for slot in range(run):
+            tile = table[window_of(slot), :, pl.ds(start, TILE)]
+            for field in range(FIELDS):
+                bufs[slot][(grp * own + block) * FIELDS + field] = tile[field : field + 1]
+        return carry
+
+    lax.fori_loop(0, own, pack, 0)
 
     shares = []
     lowers = []
@@ -134,7 +141,7 @@
     counts = [0] * run
 
     def share_of(slot, owner):
-        return bufs[slot].at[pl.ds(owner * own, own)]
+        return bufs[slot].at[pl.ds(owner * (own * FIELDS), own * FIELDS)]
 
     def descriptor(slot, owner, target, number):
         return pltpu.make_async_remote_copy(
@@ -202,7 +209,7 @@
 
     def lambda_list(slot):
         window = win * run + window_of(slot)
-        if two_ends and slot == 0:
+        if two_ends and slot == 1:
             low = jnp.where(window == 0, 0, window - 1)
             return [lambdas[low], lambdas[low + 1]]
         return [
@@ -226,12 +233,13 @@
         def one(pair, state):
             row_id = row_ids[local, pair]
             col_id = col_ids[local, pair]
-            col = bufs[slot][col_id]
+            first_row = col_id * FIELDS
+            col = [bufs[slot][first_row + f] for f in range(FIELDS)]
             mine = jnp.clip(row_id - base, 0, own - 1) * (FIELDS * PIECES)
-            fields = [jnp.broadcast_to(col[f : f + 1], (ROWS, TILE)) for f in range(3)]
-            charge_col = col[3:4]
-            depth_col = col[4:5]
-            size_col = jnp.broadcast_to(1.0 / col[5:6], (ROWS, TILE))
+            fields = [jnp.broadcast_to(col[f], (ROWS, TILE)) for f in range(3)]
+            charge_col = col[3]
+            depth_col = col[4]
+            size_col = jnp.broadcast_to(1.0 / col[5], (ROWS, TILE))
             sum_disp = [None] * len(lams)
             sum_coul = [None] * len(lams)
             for piece in range(TILE // ROWS):
@@ -274,18 +282,20 @@
             own_pairs = state[-2] * (4.0 * inverse * (inverse - 1.0)) + state[-1] * lax.rsqrt(soft)
             line = jnp.sum(state[k], axis=0, keepdims=True) - own_pairs
             out.append(jnp.sum(line, axis=1, keepdims=True) * lam)
-        if two_ends and slot == 0:
+        if two_ends and slot == 1:
             out = [out[0], jnp.where(win == 0, out[0], out[1]), out[1]]
         return out
 
     open_sends(0)
+    spread(0)
+    pass_column(0)
+    for slot in range(1, run):
+        open_sends(slot)
+    pass_planes(0)
+    if run > 1:
+        pass_column(1)
     for slot in range(1, run):
         spread(slot)
-        open_sends(slot)
-    pass_column(0)
-    if run > 1:
-        pass_column(1)
-    pass_planes(0)
     last_arrivals(0)
     partial = []
     for slot in range(run):
@@ -380,7 +390,7 @@
     smem = pl.BlockSpec(memory_space=pltpu.SMEM)
     vmem = pl.BlockSpec(memory_space=pltpu.VMEM)
     devices = wins * groups
-    scratch = [pltpu.VMEM((groups * own, fields, TILE), jnp.float32) for _ in range(run)]
+    scratch = [pltpu.VMEM((groups * own * fields, 1, TILE), jnp.float32) for _ in range(run)]
     scratch += [pltpu.VMEM((own * FIELDS * PIECES, ROWS, TILE), jnp.float32) for _ in range(run)]
     scratch += [
         pltpu.VMEM((devices, 1, TILE), jnp.float32),

time: 46.9 us -> 46 us (0.981)
  Pallas kernels: 42.2 us -> 41.3 us
    pallas_call x1, Pallas kernels: 42.2 us -> 41.3 us  [per_device(): pl.pallas_call(functools.partial(kernel, cfg), out_shape=(jax.ShapeDtypeS...]
where the time goes in v2:
time: 46 us; the launch traced here: 45.8 us
  Pallas kernels  41.3 us (90%)
  local copies, waits for them, and re-layouts  2.53 us (5%)
  between operations  2 us (4%)
    pallas_call x1, Pallas kernels, per_device(): pl.pallas_call(functools.partial(kernel, cfg), out_shape=(jax.ShapeDtypeS...  41.3 us
    unnamed x12, local copies, waits for them, and re-layouts  2.53 us

profile of v2, /device:TPU:0, one launch (start us, length us, event | category | flops | bytes accessed | tf_op | source)
XLA Modules:
  0.0 45.8 jit_solution(14168620557738078063)
XLA Ops:
  1.9 0.0 copy-start
  1.9 0.0 copy-start.1
  1.9 0.0 copy-start.2
  2.0 0.0 copy-start.3
  2.0 0.9 %copy.10.table = f32[2,6,1536]{2,1,0:T(8,128)S(1)} copy(f32[2,6,1536]{2,0,1:T(2,128)} %param.7) | data formatting | bytes 147456 | tf_op args[0]
  2.9 0.0 copy-done
  2.9 0.0 copy-done.1
  2.9 0.0 copy-done.2
  2.9 0.0 copy-done.3
  2.9 41.3 %shard_map.94 = (f32[2,3]{1,0:T(2,128)S(1)}, f32[2]{0:T(128)S(1)}, f32[2]{0:T(128)S(1)}) custom-call(f32[2,6,1536]{2,1,0:T(8,128)S(1)} %copy.10.table, s32[2,64]{1,0:T(2,128)S(1)} %copy-done, s32[2,64]{1,0:T(2,128)S(1)} %copy-done.1, f32[4]{0:T(128)S(1)} %copy-done.2, f32[1]{0:T(128)S(6)} %copy.14.inverse_temp, s32[1]{0:T(128)S(6)} %copy.15.parity, ...), custom_call_target="tpu_custom_call" | custom-call | tf_op jit(solution)/shard_map/pallas_call | solution.py:402
  44.3 0.6 %copy.16 = f32[2,3]{1,0:T(2,128)} copy(f32[2,3]{1,0:T(2,128)S(1)} %get-tuple-element.6) | data formatting | bytes 48
  44.8 0.5 %copy.17 = f32[2]{0:T(128)} copy(f32[2]{0:T(128)S(1)} %get-tuple-element.7) | data formatting | bytes 16
  45.3 0.5 %copy.18 = f32[2]{0:T(128)} copy(f32[2]{0:T(128)S(1)} %get-tuple-element.8) | data formatting | bytes 16
Async XLA Ops:
  1.9 1.0 %copy-start = (s32[2,64]{1,0:T(2,128)S(1)}, s32[2,64]{1,0:T(2,128)}, u32[]{:S(2)}) copy-start(s32[2,64]{1,0:T(2,128)} %row_ids.1) | copy-start | bytes 1540
  1.9 1.0 %copy-start.1 = (s32[2,64]{1,0:T(2,128)S(1)}, s32[2,64]{1,0:T(2,128)}, u32[]{:S(2)}) copy-start(s32[2,64]{1,0:T(2,128)} %col_ids.1) | copy-start | bytes 1540
  1.9 1.0 %copy-start.2 = (f32[4]{0:T(128)S(1)}, f32[4]{0:T(128)}, u32[]{:S(2)}) copy-start(f32[4]{0:T(128)} %lambdas.1) | copy-start | bytes 52
  2.0 1.0 %copy-start.3 = (s32[4]{0:T(128)S(1)}, s32[4]{0:T(128)}, u32[]{:S(2)}) copy-start(s32[4]{0:T(128)} %thresholds.1) | copy-start | bytes 52
